TPU v7x, 32 devices: a whole 2x2x4 slice. The times are simulated.
32 devices in a mesh: group: 4 (over y, core), local: 8 (over z, x).
Axes of the slice: x: 2, y: 2, z: 4, core: 2. Of those that a mesh axis runs over, the one named last changes fastest.
Arguments:
- lookup_grads: bfloat16 [262144, 256], P(('group', 'local')), may hold values from -0.29882812 to 0.29882812
- slot_index: int32 [2, 262144], P(None, ('group', 'local')), may hold values from 0 to 511, as said below
- unique_rows: int32 [2, 2048], P(None, ('group', 'local')), may hold values from -1 to 32767, as said below
- tables: float32 [2, 32768, 256], P(None, ('group', 'local')), may hold values from -6 to 6
- accums: float32 [2, 32768], P(None, ('group', 'local')), may hold values from 0.01 to 1
Outputs:
- new_tables: float32 [2, 32768, 256], P(None, ('group', 'local'))
- new_accums: float32 [2, 32768], P(None, ('group', 'local'))
Inputs may be any that keep to these rules, and one draw needn't show every extreme that they name: slot_index[t, i] names a slot of lookup i's group list whose entry in unique_rows[t] is not -1. `unique_rows`: table row p is owned by device p // 1024, which is device (group p // 8192, local p // 1024 % 8). Group g's list is entries g * 512 to (g + 1) * 512 - 1; its block l of 64 entries consists of 4 buckets of 16 entries, bucket h holding only rows owned by device (group h, local l), the used entries first and -1 after them. Rows within a group's list are distinct. In every draw and table some device (group h, local l) gets a full bucket from every group.
All inputs are finite; a program needn't handle non-finite values.
Results may differ from a plain program's by a relative error of at most 0.0003.
Values sent between devices are 32-bit elements; how exact they have to be, the bound alone decides.
A program may use at most 64 MiB of HBM per device.

v0:
```python
import jax
import jax.numpy as jnp
from jax import lax
from jax.sharding import PartitionSpec as P

learning_rate = 0.1
epsilon = 1e-08


def slot_sums(lookup_grads, slot_index, row_count):
    block_len = min(2048, lookup_grads.shape[0])
    block_count = lookup_grads.shape[0] // block_len
    width = lookup_grads.shape[1]
    grad_blocks = lookup_grads.reshape(block_count, block_len, width)
    index_blocks = jnp.transpose(slot_index.reshape(2, block_count, block_len), (1, 0, 2))
    targets = lax.iota(jnp.int32, row_count)

    def accumulate(running, inputs):
        gradients, indices = inputs
        pieces = []
        for table_index in range(2):
            onehot = (indices[table_index][:, None] == targets[None, :]).astype(jnp.bfloat16)
            pieces.append(
                lax.dot_general(
                    onehot, gradients, (((0,), (0,)), ((), ())), preferred_element_type=jnp.float32
                )
            )
        return (running + jnp.concatenate(pieces, axis=1), None)

    start_sums = jnp.zeros((row_count, 2 * width), jnp.float32)
    summed, _ = lax.scan(accumulate, start_sums, (grad_blocks, index_blocks))
    return summed


def apply_update(summed, row_pairs, tables, accums):
    rows_dev = tables.shape[1]
    width = tables.shape[2]
    new_tables = []
    new_accums = []
    for table_index in range(2):
        row_numbers = row_pairs[:, table_index]
        local_rows = jnp.where(row_numbers < 0, rows_dev, row_numbers % rows_dev)
        values = summed[:, table_index * width : (table_index + 1) * width]
        row_grads = (
            jnp.zeros((rows_dev, width), jnp.float32).at[local_rows].add(values, mode="drop")
        )
        accum_new = accums[table_index] + jnp.mean(row_grads * row_grads, axis=1)
        table_new = tables[table_index] - learning_rate * row_grads / (
            jnp.sqrt(accum_new)[:, None] + epsilon
        )
        new_tables.append(table_new)
        new_accums.append(accum_new)
    return (jnp.stack(new_tables), jnp.stack(new_accums))


def local(lookup_grads, slot_index, unique_rows, tables, accums):
    n_group = lax.axis_size("group")
    n_local = lax.axis_size("local")
    slots = unique_rows.shape[1]
    capacity = slots // n_group
    width = lookup_grads.shape[1]
    row_pairs = jnp.transpose(unique_rows)
    own_sums = slot_sums(lookup_grads, slot_index, slots * n_local)
    ordered = own_sums.reshape(n_local, n_group, capacity, 2 * width)
    ordered = jnp.transpose(ordered, (1, 0, 2, 3)).reshape(n_local * slots, 2 * width)
    received = lax.all_to_all(ordered, ("group", "local"), split_axis=0, concat_axis=0, tiled=True)
    arrived = jnp.sum(received.reshape(n_group, n_local, capacity, 2 * width), axis=1).reshape(
        slots, 2 * width
    )
    arrived_rows = lax.all_to_all(row_pairs, "group", split_axis=0, concat_axis=0, tiled=True)
    return apply_update(arrived, arrived_rows, tables, accums)


def solution(mesh):
    return jax.shard_map(
        local,
        mesh=mesh,
        in_specs=(
            P(("group", "local"), None),
            P(None, ("group", "local")),
            P(None, ("group", "local")),
            P(None, ("group", "local"), None),
            P(None, ("group", "local")),
        ),
        out_specs=(P(None, ("group", "local"), None), P(None, ("group", "local"))),
        check_vma=False,
    )
```

profile of v0, /device:TPU:0, one launch (start us, length us, event | category | flops | bytes accessed | tf_op | source)
XLA Modules:
  0.0 72.4 jit_solution(2092852050959643658)
XLA Ops:
  0.6 0.8 %all_to_all.14 = s32[4,16,2]{1,0,2:T(4,128)S(1)} reshape(s32[64,2]{0,1:T(2,128)} %bitcast.61) | data formatting | bytes 1024 | tf_op jit(solution)/shard_map/all_to_all | solution.py:70
  1.4 0.6 copy.9
  2.0 4.3 %all-to-all-start = ((s32[4,16,2]{1,2,0:T(2,128)}), s32[4,16,2]{1,2,0:T(2,128)S(1)}, u32[]{:S(2)}, u32[]{:S(2)}) async-start(s32[4,16,2]{1,2,0:T(2,128)} %copy.9), calls=%async_computation | async-start | bytes 8192 | tf_op jit(solution)/shard_map/all_to_all | solution.py:70
  6.3 23.5 %while.12 = (s32[]{:T(128)}, f32[512,512]{0,1:T(8,128)S(1)}, s32[4,2,2048]{2,1,0:T(2,128)}, bf16[4,2048,256]{2,1,0:T(8,128)(2,1)}, s32[]{:T(128)}, /*index=5*/s32[]{:T(128)}, s32[]{}) while((s32[]{:T(128)}, f32[512,512]{0,1:T(8,128)S(1)}, s32[4,2,2048]{2,1,0:T(2,128)}, bf16[4,2048,256]{2,1,0:T(8,128)(2,1)}, s32[]{:T(128)}, ...), condition=%wide.region_1.2_spmd.clone.clone, body=%wide.region_0.1_spmd.clone.clone.sunk | while | flops 1076625408 | bytes 6340731 | solution.py:31
  6.3 0.8 %constant_dynamic-slice_fusion.3 = (s32[1,1,2048]{2,1,0:T(1,128)S(1)}, s32[1,1,2048]{2,1,0:T(1,128)S(1)}) fusion(s32[4,2,2048]{2,1,0:T(2,128)} %get-tuple-element.129, s32[]{:T(128)S(6)} %copy.15, s32[]{:T(128)S(6)} %add.113), kind=kLoop, calls=%fused_computation.15.clone.1 | loop fusion | bytes 32776 | tf_op jit(solution)/shard_map/while/body/eval_jaxpr/slice | solution.py:22
  7.1 2.3 %fusion.31 = f32[512,256]{0,1:T(8,128)S(1)} fusion(s32[2048]{0:T(1024)S(1)} %bitcast.55, bf16[4,2048,256]{2,1,0:T(8,128)(2,1)} %get-tuple-element.130, s32[]{:T(128)S(6)} %copy.15), kind=kOutput, calls=%fused_computation.5.clone.1 | convolution fusion | flops 537919488 | bytes 1581060 | tf_op jit(solution)/shard_map/while/body/eval_jaxpr/dot_general | solution.py:24
  9.4 2.3 %fusion.30 = f32[512,256]{0,1:T(8,128)S(1)} fusion(s32[2048]{0:T(1024)S(1)} %bitcast.54, bf16[4,2048,256]{2,1,0:T(8,128)(2,1)} %get-tuple-element.130, s32[]{:T(128)S(6)} %copy.15), kind=kOutput, calls=%fused_computation.6.clone.1 | convolution fusion | flops 537919488 | bytes 1581060 | tf_op jit(solution)/shard_map/while/body/eval_jaxpr/dot_general | solution.py:24
  11.7 0.4 maximum_add_fusion.2
  12.1 0.8 %constant_dynamic-slice_fusion.3 = (s32[1,1,2048]{2,1,0:T(1,128)S(1)}, s32[1,1,2048]{2,1,0:T(1,128)S(1)}) fusion(s32[4,2,2048]{2,1,0:T(2,128)} %get-tuple-element.129, s32[]{:T(128)S(6)} %copy.15, s32[]{:T(128)S(6)} %add.113), kind=kLoop, calls=%fused_computation.15.clone.1 | loop fusion | bytes 32776 | tf_op jit(solution)/shard_map/while/body/eval_jaxpr/slice | solution.py:22
  12.9 2.3 %fusion.31 = f32[512,256]{0,1:T(8,128)S(1)} fusion(s32[2048]{0:T(1024)S(1)} %bitcast.55, bf16[4,2048,256]{2,1,0:T(8,128)(2,1)} %get-tuple-element.130, s32[]{:T(128)S(6)} %copy.15), kind=kOutput, calls=%fused_computation.5.clone.1 | convolution fusion | flops 537919488 | bytes 1581060 | tf_op jit(solution)/shard_map/while/body/eval_jaxpr/dot_general | solution.py:24
  15.3 2.3 %fusion.30 = f32[512,256]{0,1:T(8,128)S(1)} fusion(s32[2048]{0:T(1024)S(1)} %bitcast.54, bf16[4,2048,256]{2,1,0:T(8,128)(2,1)} %get-tuple-element.130, s32[]{:T(128)S(6)} %copy.15), kind=kOutput, calls=%fused_computation.6.clone.1 | convolution fusion | flops 537919488 | bytes 1581060 | tf_op jit(solution)/shard_map/while/body/eval_jaxpr/dot_general | solution.py:24
  17.6 0.4 maximum_add_fusion.2
  18.0 0.8 %constant_dynamic-slice_fusion.3 = (s32[1,1,2048]{2,1,0:T(1,128)S(1)}, s32[1,1,2048]{2,1,0:T(1,128)S(1)}) fusion(s32[4,2,2048]{2,1,0:T(2,128)} %get-tuple-element.129, s32[]{:T(128)S(6)} %copy.15, s32[]{:T(128)S(6)} %add.113), kind=kLoop, calls=%fused_computation.15.clone.1 | loop fusion | bytes 32776 | tf_op jit(solution)/shard_map/while/body/eval_jaxpr/slice | solution.py:22
  18.8 2.3 %fusion.31 = f32[512,256]{0,1:T(8,128)S(1)} fusion(s32[2048]{0:T(1024)S(1)} %bitcast.55, bf16[4,2048,256]{2,1,0:T(8,128)(2,1)} %get-tuple-element.130, s32[]{:T(128)S(6)} %copy.15), kind=kOutput, calls=%fused_computation.5.clone.1 | convolution fusion | flops 537919488 | bytes 1581060 | tf_op jit(solution)/shard_map/while/body/eval_jaxpr/dot_general | solution.py:24
  21.2 2.3 %fusion.30 = f32[512,256]{0,1:T(8,128)S(1)} fusion(s32[2048]{0:T(1024)S(1)} %bitcast.54, bf16[4,2048,256]{2,1,0:T(8,128)(2,1)} %get-tuple-element.130, s32[]{:T(128)S(6)} %copy.15), kind=kOutput, calls=%fused_computation.6.clone.1 | convolution fusion | flops 537919488 | bytes 1581060 | tf_op jit(solution)/shard_map/while/body/eval_jaxpr/dot_general | solution.py:24
  23.5 0.4 maximum_add_fusion.2
  23.9 0.8 %constant_dynamic-slice_fusion.3 = (s32[1,1,2048]{2,1,0:T(1,128)S(1)}, s32[1,1,2048]{2,1,0:T(1,128)S(1)}) fusion(s32[4,2,2048]{2,1,0:T(2,128)} %get-tuple-element.129, s32[]{:T(128)S(6)} %copy.15, s32[]{:T(128)S(6)} %add.113), kind=kLoop, calls=%fused_computation.15.clone.1 | loop fusion | bytes 32776 | tf_op jit(solution)/shard_map/while/body/eval_jaxpr/slice | solution.py:22
  24.7 2.3 %fusion.31 = f32[512,256]{0,1:T(8,128)S(1)} fusion(s32[2048]{0:T(1024)S(1)} %bitcast.55, bf16[4,2048,256]{2,1,0:T(8,128)(2,1)} %get-tuple-element.130, s32[]{:T(128)S(6)} %copy.15), kind=kOutput, calls=%fused_computation.5.clone.1 | convolution fusion | flops 537919488 | bytes 1581060 | tf_op jit(solution)/shard_map/while/body/eval_jaxpr/dot_general | solution.py:24
  27.1 2.3 %fusion.30 = f32[512,256]{0,1:T(8,128)S(1)} fusion(s32[2048]{0:T(1024)S(1)} %bitcast.54, bf16[4,2048,256]{2,1,0:T(8,128)(2,1)} %get-tuple-element.130, s32[]{:T(128)S(6)} %copy.15), kind=kOutput, calls=%fused_computation.6.clone.1 | convolution fusion | flops 537919488 | bytes 1581060 | tf_op jit(solution)/shard_map/while/body/eval_jaxpr/dot_general | solution.py:24
  29.4 0.4 maximum_add_fusion.2
  29.8 0.3 copy.11
  30.1 1.0 %copy.12 = f32[4,8,16,512]{3,2,1,0:T(8,128)} copy(f32[4,8,16,512]{3,2,0,1:T(8,128)S(1)} %bitcast.51) | data formatting | bytes 2097152 | tf_op jit(solution)/shard_map/transpose | solution.py:65
  31.2 0.0 copy-start
  31.2 0.0 all-to-all-done
  31.2 6.8 %all-to-all-start.1 = ((f32[32,16,512]{2,1,0:T(8,128)}), f32[32,16,512]{2,1,0:T(8,128)S(1)}, u32[]{:S(2)}, u32[]{:S(2)}) async-start(f32[32,16,512]{2,1,0:T(8,128)} %bitcast.8), calls=%async_computation.1 | async-start | bytes 2097152 | tf_op jit(solution)/shard_map/all_to_all | solution.py:66
  38.0 0.1 all_to_all.16
  38.1 27.4 %all-to-all-done.1 = f32[32,16,512]{2,1,0:T(8,128)S(1)} async-done(((f32[32,16,512]{2,1,0:T(8,128)}), f32[32,16,512]{2,1,0:T(8,128)S(1)}, u32[]{:S(2)}, u32[]{:S(2)}) %all-to-all-start.1) | async-done | bytes 1048608 | tf_op jit(solution)/shard_map/all_to_all | solution.py:66
  65.4 0.1 bitcast_reduce_fusion
  65.5 1.2 %scatter_custom_fusion.1 = f32[1024,256]{1,0:T(8,128)S(1)} fusion(s32[64]{0:T(128)S(1)} %get-tuple-element.81, f32[]{:T(128)} %constant.37.clone.1, f32[64,512]{1,0:T(8,128)S(1)} %bitcast.52), kind=kCustom, calls=%fused_computation.26 | custom fusion | flops 16384 | bytes 1114116 | tf_op jit(solution)/shard_map/scatter-add | solution.py:45
  66.7 0.2 multiply_reduce_fusion
  66.9 1.2 %scatter_custom_fusion = f32[1024,256]{1,0:T(8,128)S(1)} fusion(s32[64]{0:T(128)S(1)} %get-tuple-element.80, f32[]{:T(128)} %constant.37.clone.1, f32[64,512]{1,0:T(8,128)S(1)} %bitcast.53), kind=kCustom, calls=%fused_computation.28 | custom fusion | flops 16384 | bytes 1114116 | tf_op jit(solution)/shard_map/scatter-add | solution.py:45
  68.1 0.2 multiply_reduce_fusion.1
  68.4 0.0 copy-done
  68.4 0.6 pad_maximum_fusion.1
  69.0 1.9 %fusion.13 = (f32[1,1024,256]{2,1,0:T(8,128)S(1)}, f32[1,1024,256]{2,1,0:T(8,128)S(1)}) fusion(f32[1024,256]{1,0:T(8,128)S(1)} %scatter_custom_fusion, f32[2,1024,256]{2,1,0:T(8,128)} %param.10, f32[1024]{0:T(1024)S(1)} %get-tuple-element.83, f32[1024]{0:T(1024)S(1)} %get-tuple-element.82, f32[1024,256]{1,0:T(8,128)S(1)} %scatter_custom_fusion.1), kind=kLoop, calls=%fused_computation.23 | loop fusion | flops 1572864 | bytes 6299648 | tf_op jit(solution)/shard_map/stack | solution.py:53
  70.9 1.5 %pad_maximum_fusion = f32[2,1024,256]{2,1,0:T(8,128)} fusion(f32[1,1024,256]{2,1,0:T(8,128)S(1)} %get-tuple-element.75, f32[1,1024,256]{2,1,0:T(8,128)S(1)} %get-tuple-element.74), kind=kLoop, calls=%fused_computation.18 | loop fusion | flops 524288 | bytes 4194304 | tf_op jit(solution)/shard_map/stack | solution.py:53
  (7 shorter events, 0.1 us)
Async XLA Ops:
  2.0 29.2 %all-to-all-start = ((s32[4,16,2]{1,2,0:T(2,128)}), s32[4,16,2]{1,2,0:T(2,128)S(1)}, u32[]{:S(2)}, u32[]{:S(2)}) async-start(s32[4,16,2]{1,2,0:T(2,128)} %copy.9), calls=%async_computation | async-start | bytes 8192 | tf_op jit(solution)/shard_map/all_to_all | solution.py:70
  31.2 37.2 %copy-start = (f32[2,1024]{1,0:T(2,128)S(1)}, f32[2,1024]{1,0:T(2,128)}, u32[]{:S(2)}) copy-start(f32[2,1024]{1,0:T(2,128)} %param.11) | copy-start | bytes 24580
  31.2 34.3 %all-to-all-start.1 = ((f32[32,16,512]{2,1,0:T(8,128)}), f32[32,16,512]{2,1,0:T(8,128)S(1)}, u32[]{:S(2)}, u32[]{:S(2)}) async-start(f32[32,16,512]{2,1,0:T(8,128)} %bitcast.8), calls=%async_computation.1 | async-start | bytes 2097152 | tf_op jit(solution)/shard_map/all_to_all | solution.py:66
where the time goes:
time: 73.4 us; the launch traced here: 72.4 us
  waiting for transfers between devices  27.4 us (37%)
  matrix products  18.7 us (25%)
  starting transfers between devices  11 us (15%)
  other arithmetic  8.34 us (11%)
  local copies, waits for them, and re-layouts  6.07 us (8%)
  between operations  0.74 us (1%)
    all_to_all x1, waiting for transfers between devices, local(): lax.all_to_all(ordered, ('group', 'local'), split_axis=0, concat_axis=0,...  27.4 us
    dot_general x8, matrix products, accumulate(): lax.dot_general(onehot, gradients, (((0,), (0,)), ((), ())), preferred_el...  18.7 us
    all_to_all x1, starting transfers between devices, local(): lax.all_to_all(ordered, ('group', 'local'), split_axis=0, concat_axis=0,...  6.78 us
    all_to_all x1, starting transfers between devices, local(): lax.all_to_all(row_pairs, 'group', split_axis=0, concat_axis=0, tiled=True)  4.26 us
    another operation x3, other arithmetic, apply_update(): return (jnp.stack(new_tables), jnp.stack(new_accums))  3.98 us
    slice x4, local copies, waits for them, and re-layouts, accumulate(): indices[table_index][:, None] == targets[None, :]  3.25 us
    scatter-add x2, other arithmetic, apply_update(): jnp.zeros((rows_dev, width), jnp.float32).at[local_rows]  2.37 us
  transfers between devices with their start and end apart: 2, of which 1 were waited for; matrix products, arithmetic and copies ran while one was open for 34% of the time, Pallas kernels for 0%

commit v1 on v0

v1 whole, which is shorter than its diff:
```python
import functools

import jax
import jax.numpy as jnp
from jax import lax
from jax.experimental import pallas as pl
from jax.experimental.pallas import tpu as pltpu
from jax.sharding import PartitionSpec as P

learning_rate = 0.1
epsilon = 1e-08
MESH = pl.DeviceIdType.MESH
BLOCKS = 4


def exchange_kernel(
    n_group, n_local, chunk, grads_hbm, index_ref, rows_ref, arrived_ref, rows_out_ref,
    grads, sums, recv, rows_recv, acc, grad_sems, send_sem, recv_sem, row_send_sem, row_recv_sem,
):
    group, local = lax.axis_index("group"), lax.axis_index("local")
    n_dev = n_group * n_local
    me = group * n_local + local
    look, width = grads.shape
    capacity = sums.shape[2]
    n_chunk = look // chunk
    locals_block = n_local // BLOCKS
    buckets = locals_block * n_group
    rows_block = buckets * capacity

    def load(k):
        at = pl.ds(k * chunk, chunk)
        return pltpu.make_async_copy(grads_hbm.at[at], grads.at[at], grad_sems.at[k])

    for k in range(n_chunk):
        load(k).start()

    barrier = pltpu.get_barrier_semaphore()

    def greet(o, c):
        to = lax.rem(me + o, n_dev)
        pl.semaphore_signal(
            barrier, inc=1, device_id={"group": to // n_local, "local": lax.rem(to, n_local)},
            device_id_type=MESH,
        )
        return c

    lax.fori_loop(1, n_dev, greet, 0)

    def send_bucket(bucket, l, h):
        return pltpu.make_async_remote_copy(
            src_ref=sums.at[bucket], dst_ref=recv.at[me],
            send_sem=send_sem, recv_sem=recv_sem,
            device_id={"group": h, "local": l}, device_id_type=MESH,
        )

    def send_rows(h):
        return pltpu.make_async_remote_copy(
            src_ref=rows_ref, dst_ref=rows_recv.at[group],
            send_sem=row_send_sem, recv_sem=row_recv_sem,
            device_id={"group": h, "local": local}, device_id_type=MESH,
        )

    block_me = local // locals_block
    for step in range(BLOCKS):
        block = lax.rem(block_me + (2, 1, 3, 0)[step], BLOCKS)
        targets = lax.broadcasted_iota(jnp.int32, (rows_block, chunk), 0) + block * rows_block
        acc[...] = jnp.zeros_like(acc)

        def body(k, c):
            if step == 0:
                load(k).wait()
            at = pl.ds(pl.multiple_of(k * chunk, chunk), chunk)
            onehot = jnp.concatenate(
                [jnp.where(index_ref[t : t + 1, at] == targets, 1.0, 0.0).astype(jnp.bfloat16) for t in range(2)],
                axis=0,
            )
            acc[...] += jnp.dot(onehot, grads[at, :], preferred_element_type=jnp.float32)
            return c

        lax.fori_loop(0, n_chunk, body, 0)
        first = block * buckets
        for t in range(2):
            sums[pl.ds(first, buckets), t] = acc[t * rows_block : (t + 1) * rows_block, :].reshape(
                buckets, capacity, width
            )
        if step == 0:
            pl.semaphore_wait(barrier, n_dev - 1)

            def row_step(o, c):
                send_rows(lax.rem(group + o, n_group)).start()
                return c

            lax.fori_loop(1, n_group, row_step, 0)

        if step < BLOCKS - 1:

            def out_step(i, c):
                l = block * locals_block + lax.rem(local + i // n_group, locals_block)
                h = lax.rem(group + i, n_group)
                send_bucket(l * n_group + h, l, h).start()
                return c

            lax.fori_loop(0, buckets, out_step, 0)
        else:

            def own_step(i, c):
                l = block * locals_block + lax.rem(local + i // n_group, locals_block)
                h = lax.rem(group + i, n_group)
                send_bucket(l * n_group + h, l, h).start()
                return c

            lax.fori_loop(1, buckets, own_step, 0)

    recv[me] = sums[local * n_group + group]
    rows_recv[group] = rows_ref[...]
    everyone = pltpu.make_async_remote_copy(
        src_ref=sums.at[pl.ds(0, n_dev - 1)], dst_ref=recv.at[pl.ds(0, n_dev - 1)],
        send_sem=send_sem, recv_sem=recv_sem,
        device_id={"group": group, "local": local}, device_id_type=MESH,
    )
    row_wait = pltpu.make_async_remote_copy(
        src_ref=rows_recv.at[pl.ds(0, n_group - 1)], dst_ref=rows_recv.at[pl.ds(0, n_group - 1)],
        send_sem=row_send_sem, recv_sem=row_recv_sem,
        device_id={"group": group, "local": local}, device_id_type=MESH,
    )
    row_wait.wait_recv()
    everyone.wait_recv()
    rows_out_ref[...] = rows_recv[...]
    for g in range(n_group):
        for t in range(2):
            total = recv[g * n_local, t]
            for l in range(1, n_local):
                total = total + recv[g * n_local + l, t]
            arrived_ref[t, g * capacity : (g + 1) * capacity, :] = total
    row_wait.wait_send()
    everyone.wait_send()


def update_kernel(
    n_group, rows_smem, rows_ref, arrived_ref, tables_ref, accums_ref, new_tables_ref, new_accums_ref, picked, fresh
):
    group, local = lax.axis_index("group"), lax.axis_index("local")
    n_local = lax.axis_size("local")
    rows_dev, width = tables_ref.shape[1:]
    slots = arrived_ref.shape[1]
    capacity = slots // n_group
    base = (group * n_local + local) * rows_dev
    new_tables_ref[...] = tables_ref[...]
    slot_at = lax.broadcasted_iota(jnp.int32, (capacity, slots), 0)
    lane_at = lax.broadcasted_iota(jnp.int32, (capacity, slots), 1)
    diagonal = lax.broadcasted_iota(jnp.int32, (slots, slots), 0) == lax.broadcasted_iota(jnp.int32, (slots, slots), 1)
    row_lane = lax.broadcasted_iota(jnp.int32, (slots, rows_dev), 1).astype(jnp.float32)
    for t in range(2):
        for s in range(slots):
            row = rows_smem[s // capacity, t, group * capacity + s % capacity]
            at = jnp.where(row < 0, 0, row - base)
            picked[s, :] = tables_ref[t, at, :]
        columns = []
        for g in range(n_group):
            mine = lane_at == slot_at + group * capacity
            ids = (rows_ref[g, t : t + 1, :]).astype(jnp.float32)
            columns.append(jnp.sum(jnp.where(mine, ids, 0.0), axis=1, keepdims=True))
        column = jnp.concatenate(columns, axis=0)
        as_row = jnp.sum(jnp.where(diagonal, column, 0.0), axis=0, keepdims=True)
        same = jnp.where(column == as_row, 1.0, 0.0)
        totals = jnp.dot(
            same, arrived_ref[t], preferred_element_type=jnp.float32, precision=lax.Precision.HIGHEST
        )
        squares = jnp.mean(totals * totals, axis=1, keepdims=True)
        local_row = jnp.where(column < 0.0, -1.0, column - base.astype(jnp.float32))
        hit = row_lane == local_row
        accums = accums_ref[t : t + 1, :]
        old = jnp.sum(jnp.where(hit, accums, 0.0), axis=1, keepdims=True)
        added = jnp.max(jnp.where(hit, squares, 0.0), axis=0, keepdims=True)
        new_accums_ref[t : t + 1, :] = accums + added
        fresh[...] = picked[...] - learning_rate * totals / (jnp.sqrt(old + squares) + epsilon)
        for s in range(slots):
            row = rows_smem[s // capacity, t, group * capacity + s % capacity]

            @pl.when(row >= 0)
            def _():
                new_tables_ref[t, row - base, :] = fresh[s, :]


def local_step(n_group, n_local, lookup_grads, slot_index, unique_rows, tables, accums):
    look, width = lookup_grads.shape
    slots = unique_rows.shape[1]
    capacity = slots // n_group
    n_dev = n_group * n_local
    chunk = min(1024, look)
    block_rows = 2 * (slots * n_local // BLOCKS)
    vmem = pl.BlockSpec(memory_space=pltpu.VMEM)
    dma = pltpu.SemaphoreType.DMA
    arrived, rows = pl.pallas_call(
        functools.partial(exchange_kernel, n_group, n_local, chunk),
        out_shape=(
            jax.ShapeDtypeStruct((2, slots, width), jnp.float32),
            jax.ShapeDtypeStruct((n_group, 2, slots), jnp.int32),
        ),
        in_specs=[pl.BlockSpec(memory_space=pl.ANY), vmem, vmem],
        out_specs=(vmem, vmem),
        scratch_shapes=[
            pltpu.VMEM((look, width), jnp.bfloat16),
            pltpu.VMEM((n_dev, 2, capacity, width), jnp.float32),
            pltpu.VMEM((n_dev, 2, capacity, width), jnp.float32),
            pltpu.VMEM((n_group, 2, slots), jnp.int32),
            pltpu.VMEM((block_rows, width), jnp.float32),
            dma((look // chunk,)), dma, dma, dma, dma,
        ],
        compiler_params=pltpu.CompilerParams(
            collective_id=0, has_side_effects=True, vmem_limit_bytes=40 * 2**20
        ),
        cost_estimate=pl.CostEstimate(flops=2 * 2 * look * width * slots * n_local, bytes_accessed=2 * look * width, transcendentals=0),
    )(lookup_grads, slot_index, unique_rows)
    return pl.pallas_call(
        functools.partial(update_kernel, n_group),
        out_shape=(
            jax.ShapeDtypeStruct(tables.shape, jnp.float32),
            jax.ShapeDtypeStruct(accums.shape, jnp.float32),
        ),
        in_specs=[pl.BlockSpec(memory_space=pltpu.SMEM), vmem, vmem, vmem, vmem],
        out_specs=(vmem, vmem),
        scratch_shapes=[pltpu.VMEM((slots, width), jnp.float32)] * 2,
        compiler_params=pltpu.CompilerParams(vmem_limit_bytes=24 * 2**20),
    )(rows, rows, arrived, tables, accums)


def solution(mesh):
    n_group, n_local = mesh.shape["group"], mesh.shape["local"]
    return jax.shard_map(
        functools.partial(local_step, n_group, n_local),
        mesh=mesh,
        in_specs=(
            P(("group", "local"), None),
            P(None, ("group", "local")),
            P(None, ("group", "local")),
            P(None, ("group", "local"), None),
            P(None, ("group", "local")),
        ),
        out_specs=(P(None, ("group", "local"), None), P(None, ("group", "local"))),
        check_vma=False,
    )
```

time: 73.4 us -> 39.6 us (0.54)
  Pallas kernels: 0 us -> 34.5 us
  waiting for transfers between devices: 27.4 us -> 0 us
  matrix products: 18.7 us -> 0 us
  starting transfers between devices: 11 us -> 0 us
  other arithmetic: 8.34 us -> 0 us
  local copies, waits for them, and re-layouts: 6.07 us -> 3.86 us
    pallas_call x0 -> x2, Pallas kernels: none -> 34.5 us  [the longest x1 30 us: local_step(): pl.pallas_call(functools.partial(exchange_kernel, n_group, n_local, chunk...]
    all_to_all x2 -> x0, waiting for transfers between devices: 27.4 us -> none  [the longest x1 27.4 us: local(): lax.all_to_all(ordered, ('group', 'local'), split_axis=0, concat_axis=0,...]
    dot_general x8 -> x0, matrix products: 18.7 us -> none  [accumulate(): lax.dot_general(onehot, gradients, (((0,), (0,)), ((), ())), preferred_el...]
    all_to_all x2 -> x0, starting transfers between devices: 11 us -> none  [the longest x1 6.78 us: local(): lax.all_to_all(ordered, ('group', 'local'), split_axis=0, concat_axis=0,...]
    another operation x3 -> x0, other arithmetic: 3.98 us -> none  [apply_update(): return (jnp.stack(new_tables), jnp.stack(new_accums))]
    unnamed x2 -> x10, local copies, waits for them, and re-layouts: 0.01 us -> 3.86 us
    slice x4 -> x0, local copies, waits for them, and re-layouts: 3.25 us -> none  [accumulate(): indices[table_index][:, None] == targets[None, :]]
    scatter-add x2 -> x0, other arithmetic: 2.37 us -> none  [apply_update(): jnp.zeros((rows_dev, width), jnp.float32).at[local_rows]]
  transfers between devices with their start and end apart: 2 -> 0, of which waited for: 1 -> 0; matrix products, arithmetic and copies ran while one was open for 34% -> 0% of each run, Pallas kernels for 0% -> 0%
where the time goes in v1:
time: 39.6 us; the launch traced here: 39.1 us
  Pallas kernels  34.5 us (87%)
  local copies, waits for them, and re-layouts  3.86 us (10%)
  between operations  0.68 us (2%)
    pallas_call x1, Pallas kernels, local_step(): pl.pallas_call(functools.partial(exchange_kernel, n_group, n_local, chunk...  30 us
    pallas_call x1, Pallas kernels, local_step(): pl.pallas_call(functools.partial(update_kernel, n_group), out_shape=(jax....  4.57 us
    unnamed x10, local copies, waits for them, and re-layouts  3.86 us

profile of v1, /device:TPU:0, one launch (start us, length us, event | category | flops | bytes accessed | tf_op | source)
XLA Modules:
  0.0 39.1 jit_solution(7208977298850482357)
XLA Ops:
  0.6 0.0 copy-start.1
  0.6 0.0 copy-start
  0.7 0.0 copy-start.2
  0.7 2.3 %copy-done.2 = bf16[8192,256]{1,0:T(8,128)(2,1)S(1)} copy-done((bf16[8192,256]{1,0:T(8,128)(2,1)S(1)}, bf16[8192,256]{1,0:T(8,128)(2,1)}, u32[]{:S(2)}) %copy-start.2) | copy-done | bytes 4194328
  3.0 0.0 copy-start.3
  3.0 0.8 %copy-done.3 = s32[2,8192]{1,0:T(2,128)S(1)} copy-done((s32[2,8192]{1,0:T(2,128)S(1)}, s32[2,8192]{1,0:T(2,128)}, u32[]{:S(2)}) %copy-start.3) | copy-done | bytes 65560
  3.8 0.0 copy-start.4
  3.8 0.7 %copy-done.4 = s32[2,64]{1,0:T(2,128)S(1)} copy-done((s32[2,64]{1,0:T(2,128)S(1)}, s32[2,64]{1,0:T(2,128)}, u32[]{:S(2)}) %copy-start.4) | copy-done | bytes 536
  4.5 30.0 %shard_map.68 = (f32[2,64,256]{2,1,0:T(8,128)S(1)}, s32[4,2,64]{2,1,0:T(2,128)S(1)}) custom-call(bf16[8192,256]{1,0:T(8,128)(2,1)S(1)} %copy-done.2, s32[2,8192]{1,0:T(2,128)S(1)} %copy-done.3, s32[2,64]{1,0:T(2,128)S(1)} %copy-done.4), custom_call_target="tpu_custom_call" | custom-call | flops 4294967296 | bytes 4194304 | tf_op jit(solution)/shard_map/pallas_call | solution.py:194
  34.5 0.0 copy-done.1
  34.5 0.0 copy-done
  34.5 4.6 %shard_map.69 = (f32[2,1024,256]{2,1,0:T(8,128)}, f32[2,1024]{1,0:T(2,128)}) custom-call(s32[4,2,64]{2,1,0:T(2,128)S(1)} %get-tuple-element.4.rows_smem.rows_ref, s32[4,2,64]{2,1,0:T(2,128)S(1)} %get-tuple-element.4.rows_smem.rows_ref, f32[2,64,256]{2,1,0:T(8,128)S(1)} %get-tuple-element.5.arrived_ref, f32[2,1024,256]{2,1,0:T(8,128)S(1)} %copy-done, ...), custom_call_target="tpu_custom_call" | custom-call | tf_op jit(solution)/shard_map/pallas_call | solution.py:215
Async XLA Ops:
  0.6 33.9 %copy-start.1 = (f32[2,1024]{1,0:T(2,128)S(1)}, f32[2,1024]{1,0:T(2,128)}, u32[]{:S(2)}) copy-start(f32[2,1024]{1,0:T(2,128)} %accums_ref.1) | copy-start | bytes 24580
  0.6 33.9 %copy-start = (f32[2,1024,256]{2,1,0:T(8,128)S(1)}, f32[2,1024,256]{2,1,0:T(8,128)}, u32[]{:S(2)}) copy-start(f32[2,1024,256]{2,1,0:T(8,128)} %tables_ref.1) | copy-start | bytes 6291460
  0.7 2.3 %copy-start.2 = (bf16[8192,256]{1,0:T(8,128)(2,1)S(1)}, bf16[8192,256]{1,0:T(8,128)(2,1)}, u32[]{:S(2)}) copy-start(bf16[8192,256]{1,0:T(8,128)(2,1)} %grads_hbm.1) | copy-start | bytes 12582916
  3.0 0.8 %copy-start.3 = (s32[2,8192]{1,0:T(2,128)S(1)}, s32[2,8192]{1,0:T(2,128)}, u32[]{:S(2)}) copy-start(s32[2,8192]{1,0:T(2,128)} %index_ref.1) | copy-start | bytes 196612
  3.8 0.7 %copy-start.4 = (s32[2,64]{1,0:T(2,128)S(1)}, s32[2,64]{1,0:T(2,128)}, u32[]{:S(2)}) copy-start(s32[2,64]{1,0:T(2,128)} %rows_ref.1) | copy-start | bytes 1540

commit v2 on v1

v2 whole, which is shorter than its diff:
```python
import functools

import jax
import jax.numpy as jnp
from jax import lax
from jax.experimental import pallas as pl
from jax.experimental.pallas import tpu as pltpu
from jax.sharding import PartitionSpec as P

learning_rate = 0.1
epsilon = 1e-08
MESH = pl.DeviceIdType.MESH
BLOCKS = 4


def exchange_kernel(
    n_group, n_local, chunk, grads_hbm, index_hbm, rows_hbm, arrived_ref, rows_out_ref,
    grads, index, rows, sums, pair, recv, rows_recv, acc,
    grad_sems, index_sem, rows_sem, pair_sems, pair_send_sem, send_sem, recv_sem, row_send_sem, row_recv_sem,
):
    group, local = lax.axis_index("group"), lax.axis_index("local")
    n_dev = n_group * n_local
    me = group * n_local + local
    look, width = grads.shape
    capacity = sums.shape[2]
    n_chunk = look // chunk
    peers = n_local // BLOCKS
    buckets = peers * n_group
    rows_block = buckets * capacity
    block_me, peer_me = local // peers, lax.rem(local, peers)

    index_load = pltpu.make_async_copy(index_hbm, index, index_sem)
    rows_load = pltpu.make_async_copy(rows_hbm, rows, rows_sem)

    def load(k):
        at = pl.ds(k * chunk, chunk)
        return pltpu.make_async_copy(grads_hbm.at[at], grads.at[at], grad_sems.at[k])

    index_load.start()
    for k in range(n_chunk):
        load(k).start()
    rows_load.start()

    barrier = pltpu.get_barrier_semaphore()

    def greet(o, c):
        to = lax.rem(me + o, n_dev)
        pl.semaphore_signal(
            barrier, inc=1, device_id={"group": to // n_local, "local": lax.rem(to, n_local)},
            device_id_type=MESH,
        )
        return c

    lax.fori_loop(1, n_dev, greet, 0)

    def send_pair(block, o, h):
        to = block * peers + lax.rem(peer_me + o, peers)
        return pltpu.make_async_remote_copy(
            src_ref=sums.at[to * n_group + h],
            dst_ref=pair.at[(block * n_group + h) * (peers - 1) + (peers - 1 - o)],
            send_sem=pair_send_sem, recv_sem=pair_sems.at[block * n_group + h],
            device_id={"group": group, "local": block_me * peers + lax.rem(peer_me + o, peers)},
            device_id_type=MESH,
        )

    def send_bucket(l, h, place):
        return pltpu.make_async_remote_copy(
            src_ref=sums.at[l * n_group + h], dst_ref=recv.at[group * places + place],
            send_sem=send_sem, recv_sem=recv_sem,
            device_id={"group": h, "local": l}, device_id_type=MESH,
        )

    def send_rows(h):
        return pltpu.make_async_remote_copy(
            src_ref=rows, dst_ref=rows_recv.at[group],
            send_sem=row_send_sem, recv_sem=row_recv_sem,
            device_id={"group": h, "local": local}, device_id_type=MESH,
        )

    places = BLOCKS - 1 + peers
    order = (2, 1, 3, 0)

    def block_at(step):
        return lax.rem(block_me + order[step], BLOCKS)

    def sum_block(step):
        block = block_at(step)
        targets = lax.broadcasted_iota(jnp.int32, (rows_block, chunk), 0) + block * rows_block

        def body(k, c):
            if step == 0:
                load(k).wait()
            at = pl.ds(pl.multiple_of(k * chunk, chunk), chunk)
            onehot = jnp.concatenate(
                [jnp.where(index[t : t + 1, at] == targets, 1.0, 0.0).astype(jnp.bfloat16) for t in range(2)],
                axis=0,
            )
            acc[...] += jnp.dot(onehot, grads[at, :], preferred_element_type=jnp.float32)
            return c

        acc[...] = jnp.zeros_like(acc)
        if step == 0:
            index_load.wait()
        lax.fori_loop(0, n_chunk, body, 0)
        for t in range(2):
            sums[pl.ds(block * buckets, buckets), t] = acc[t * rows_block : (t + 1) * rows_block, :].reshape(
                buckets, capacity, width
            )

    def start_pairs(step):
        def one(i, c):
            send_pair(block_at(step), 1 + i // n_group, lax.rem(group + lax.rem(i, n_group), n_group)).start()
            return c

        lax.fori_loop(0, (peers - 1) * n_group, one, 0)

    def pass_on(step):
        block = block_at(step)
        mine = block * peers + peer_me

        def one(i, c):
            h = lax.rem(group + i, n_group)
            first = (block * n_group + h) * (peers - 1)
            pltpu.make_async_remote_copy(
                src_ref=pair.at[pl.ds(first, peers - 1)], dst_ref=pair.at[pl.ds(first, peers - 1)],
                send_sem=pair_send_sem, recv_sem=pair_sems.at[block * n_group + h],
                device_id={"group": group, "local": local}, device_id_type=MESH,
            ).wait_recv()
            total = sums[mine * n_group + h]
            for p in range(peers - 1):
                total = total + pair[first + p]
            sums[mine * n_group + h] = total
            send_bucket(mine, h, order[step] - 1).start()
            return c

        lax.fori_loop(0, n_group, one, 0)

    sum_block(0)
    pl.semaphore_wait(barrier, n_dev - 1)
    start_pairs(0)
    rows_load.wait()

    def row_step(o, c):
        send_rows(lax.rem(group + o, n_group)).start()
        return c

    lax.fori_loop(1, n_group, row_step, 0)
    for step in range(1, BLOCKS - 1):
        sum_block(step)
        start_pairs(step)
    pass_on(0)
    sum_block(BLOCKS - 1)

    def own_step(i, c):
        l = block_me * peers + lax.rem(peer_me + i // n_group, peers)
        send_bucket(l, lax.rem(group + i, n_group), BLOCKS - 1 + peer_me).start()
        return c

    lax.fori_loop(1, buckets, own_step, 0)
    for step in range(1, BLOCKS - 1):
        pass_on(step)

    recv[group * places + BLOCKS - 1 + peer_me] = sums[local * n_group + group]
    rows_recv[group] = rows[...]
    parts = n_group * places - 1
    everyone = pltpu.make_async_remote_copy(
        src_ref=recv.at[pl.ds(0, parts)], dst_ref=recv.at[pl.ds(0, parts)],
        send_sem=send_sem, recv_sem=recv_sem,
        device_id={"group": group, "local": local}, device_id_type=MESH,
    )
    row_wait = pltpu.make_async_remote_copy(
        src_ref=rows_recv.at[pl.ds(0, n_group - 1)], dst_ref=rows_recv.at[pl.ds(0, n_group - 1)],
        send_sem=row_send_sem, recv_sem=row_recv_sem,
        device_id={"group": group, "local": local}, device_id_type=MESH,
    )
    row_wait.wait_recv()
    rows_out_ref[...] = rows_recv[...]
    row_wait.wait_send()
    pair_wait_parts = (BLOCKS - 1) * n_group * (peers - 1)
    pltpu.make_async_remote_copy(
        src_ref=pair.at[pl.ds(0, pair_wait_parts)], dst_ref=pair.at[pl.ds(0, pair_wait_parts)],
        send_sem=pair_send_sem, recv_sem=recv_sem,
        device_id={"group": group, "local": local}, device_id_type=MESH,
    ).wait_send()
    everyone.wait_send()
    everyone.wait_recv()
    for g in range(n_group):
        for t in range(2):
            total = recv[g * places, t]
            for p in range(1, places):
                total = total + recv[g * places + p, t]
            arrived_ref[t, g * capacity : (g + 1) * capacity, :] = total


def update_kernel(
    n_group, rows_smem, rows_ref, arrived_ref, tables_ref, accums_ref, new_tables_hbm, new_accums_ref,
    picked, fresh, new, out_sems,
):
    group, local = lax.axis_index("group"), lax.axis_index("local")
    n_local = lax.axis_size("local")
    rows_dev, width = tables_ref.shape[1:]
    slots = arrived_ref.shape[1]
    capacity = slots // n_group
    base = (group * n_local + local) * rows_dev
    slot_at = lax.broadcasted_iota(jnp.int32, (capacity, slots), 0)
    lane_at = lax.broadcasted_iota(jnp.int32, (capacity, slots), 1)
    diagonal = lax.broadcasted_iota(jnp.int32, (slots, slots), 0) == lax.broadcasted_iota(jnp.int32, (slots, slots), 1)
    row_lane = lax.broadcasted_iota(jnp.int32, (slots, rows_dev), 1).astype(jnp.float32)

    def out(t):
        return pltpu.make_async_copy(new.at[t, pl.ds(0, rows_dev)], new_tables_hbm.at[t], out_sems.at[t])

    def row_of(t, s):
        return rows_smem[s // capacity, t, group * capacity + s % capacity]

    for t in range(2):
        new[t, 0:rows_dev] = tables_ref[t]
        for s in range(slots):
            row = row_of(t, s)
            picked[t, s, :] = tables_ref[t, jnp.where(row < 0, 0, row - base), :]
    for t in range(2):
        columns = []
        for g in range(n_group):
            mine = lane_at == slot_at + group * capacity
            ids = (rows_ref[g, t : t + 1, :]).astype(jnp.float32)
            columns.append(jnp.sum(jnp.where(mine, ids, 0.0), axis=1, keepdims=True))
        column = jnp.concatenate(columns, axis=0)
        as_row = jnp.sum(jnp.where(diagonal, column, 0.0), axis=0, keepdims=True)
        same = jnp.where(column == as_row, 1.0, 0.0)
        totals = jnp.dot(
            same, arrived_ref[t], preferred_element_type=jnp.float32, precision=lax.Precision.HIGHEST
        )
        squares = jnp.mean(totals * totals, axis=1, keepdims=True)
        local_row = jnp.where(column < 0.0, -1.0, column - base.astype(jnp.float32))
        hit = row_lane == local_row
        accums = accums_ref[t : t + 1, :]
        old = jnp.sum(jnp.where(hit, accums, 0.0), axis=1, keepdims=True)
        added = jnp.max(jnp.where(hit, squares, 0.0), axis=0, keepdims=True)
        new_accums_ref[t : t + 1, :] = accums + added
        fresh[t] = picked[t] - learning_rate * totals / (jnp.sqrt(old + squares) + epsilon)
        for s in range(slots):
            row = row_of(t, s)
            new[t, jnp.where(row < 0, rows_dev, row - base), :] = fresh[t, s, :]
        out(t).start()
    for t in range(2):
        out(t).wait()


def local_step(n_group, n_local, lookup_grads, slot_index, unique_rows, tables, accums):
    look, width = lookup_grads.shape
    slots = unique_rows.shape[1]
    capacity = slots // n_group
    n_dev = n_group * n_local
    rows_dev = tables.shape[1]
    chunk = min(4096, look)
    peers = n_local // BLOCKS
    block_rows = 2 * (slots * n_local // BLOCKS)
    vmem = pl.BlockSpec(memory_space=pltpu.VMEM)
    hbm = pl.BlockSpec(memory_space=pltpu.HBM)
    dma = pltpu.SemaphoreType.DMA
    arrived, rows = pl.pallas_call(
        functools.partial(exchange_kernel, n_group, n_local, chunk),
        out_shape=(
            jax.ShapeDtypeStruct((2, slots, width), jnp.float32),
            jax.ShapeDtypeStruct((n_group, 2, slots), jnp.int32),
        ),
        in_specs=[hbm, hbm, hbm],
        out_specs=(vmem, vmem),
        scratch_shapes=[
            pltpu.VMEM((look, width), jnp.bfloat16),
            pltpu.VMEM((2, look), jnp.int32),
            pltpu.VMEM((2, slots), jnp.int32),
            pltpu.VMEM((n_dev, 2, capacity, width), jnp.float32),
            pltpu.VMEM((BLOCKS * n_group * (peers - 1), 2, capacity, width), jnp.float32),
            pltpu.VMEM((n_group * (BLOCKS - 1 + peers), 2, capacity, width), jnp.float32),
            pltpu.VMEM((n_group, 2, slots), jnp.int32),
            pltpu.VMEM((block_rows, width), jnp.float32),
            dma((look // chunk,)), dma, dma, dma((BLOCKS * n_group,)), dma, dma, dma, dma, dma,
        ],
        compiler_params=pltpu.CompilerParams(
            collective_id=0, has_side_effects=True, vmem_limit_bytes=63 * 10**6
        ),
        cost_estimate=pl.CostEstimate(flops=2 * 2 * look * width * slots * n_local, bytes_accessed=2 * look * width, transcendentals=0),
    )(lookup_grads, slot_index, unique_rows)
    return pl.pallas_call(
        functools.partial(update_kernel, n_group),
        out_shape=(
            jax.ShapeDtypeStruct(tables.shape, jnp.float32),
            jax.ShapeDtypeStruct(accums.shape, jnp.float32),
        ),
        in_specs=[pl.BlockSpec(memory_space=pltpu.SMEM), vmem, vmem, vmem, vmem],
        out_specs=(hbm, vmem),
        scratch_shapes=[
            pltpu.VMEM((2, slots, width), jnp.float32),
            pltpu.VMEM((2, slots, width), jnp.float32),
            pltpu.VMEM((2, rows_dev + 8, width), jnp.float32),
            dma((2,)),
        ],
        compiler_params=pltpu.CompilerParams(vmem_limit_bytes=24 * 2**20),
    )(rows, rows, arrived, tables, accums)


def solution(mesh):
    n_group, n_local = mesh.shape["group"], mesh.shape["local"]
    return jax.shard_map(
        functools.partial(local_step, n_group, n_local),
        mesh=mesh,
        in_specs=(
            P(("group", "local"), None),
            P(None, ("group", "local")),
            P(None, ("group", "local")),
            P(None, ("group", "local"), None),
            P(None, ("group", "local")),
        ),
        out_specs=(P(None, ("group", "local"), None), P(None, ("group", "local"))),
        check_vma=False,
    )
```

time: 39.6 us -> 30 us (0.76)
  Pallas kernels: 34.5 us -> 27.6 us
  local copies, waits for them, and re-layouts: 3.86 us -> 1.58 us
    pallas_call x1, Pallas kernels: 30 us -> 24.1 us  [local_step(): pl.pallas_call(functools.partial(exchange_kernel, n_group, n_local, chunk...]
    unnamed x10 -> x8, local copies, waits for them, and re-layouts: 3.86 us -> 1.58 us
    pallas_call x1, Pallas kernels: 4.57 us -> 3.5 us  [local_step(): pl.pallas_call(functools.partial(update_kernel, n_group), out_shape=(jax....]
where the time goes in v2:
time: 30 us; the launch traced here: 29.9 us
  Pallas kernels  27.6 us (92%)
  local copies, waits for them, and re-layouts  1.58 us (5%)
  between operations  0.68 us (2%)
    pallas_call x1, Pallas kernels, local_step(): pl.pallas_call(functools.partial(exchange_kernel, n_group, n_local, chunk...  24.1 us
    pallas_call x1, Pallas kernels, local_step(): pl.pallas_call(functools.partial(update_kernel, n_group), out_shape=(jax....  3.5 us
    unnamed x8, local copies, waits for them, and re-layouts  1.58 us

profile of v2, /device:TPU:0, one launch (start us, length us, event | category | flops | bytes accessed | tf_op | source)
XLA Modules:
  0.0 29.9 jit_solution(15906859745100810184)
XLA Ops:
  0.6 0.0 copy-start.3
  0.6 0.0 copy-start
  0.7 24.1 %shard_map.68 = (f32[2,64,256]{2,1,0:T(8,128)}, s32[4,2,64]{2,1,0:T(2,128)}) custom-call(bf16[8192,256]{1,0:T(8,128)(2,1)} %grads_hbm.1, s32[2,8192]{1,0:T(2,128)} %index_hbm.1, s32[2,64]{1,0:T(2,128)} %rows_hbm.1), custom_call_target="tpu_custom_call" | custom-call | flops 4294967296 | bytes 4194304 | tf_op jit(solution)/shard_map/pallas_call | solution.py:261
  24.8 0.0 copy-done.3
  24.8 0.0 copy-done
  24.8 0.0 copy-start.1
  24.8 0.9 %copy-done.1 = f32[2,64,256]{2,1,0:T(8,128)S(1)} copy-done((f32[2,64,256]{2,1,0:T(8,128)S(1)}, f32[2,64,256]{2,1,0:T(8,128)}, u32[]{:S(2)}) %copy-start.1) | copy-done | bytes 131096
  25.7 0.0 copy-start.2
  25.7 0.7 %copy-done.2 = s32[4,2,64]{2,1,0:T(2,128)S(1)} copy-done((s32[4,2,64]{2,1,0:T(2,128)S(1)}, s32[4,2,64]{2,1,0:T(2,128)}, u32[]{:S(2)}) %copy-start.2) | copy-done | bytes 2072
  26.4 3.5 %shard_map.69 = (f32[2,1024,256]{2,1,0:T(8,128)}, f32[2,1024]{1,0:T(2,128)}) custom-call(s32[4,2,64]{2,1,0:T(2,128)S(1)} %copy-done.2, s32[4,2,64]{2,1,0:T(2,128)S(1)} %copy-done.2, f32[2,64,256]{2,1,0:T(8,128)S(1)} %copy-done.1, f32[2,1024,256]{2,1,0:T(8,128)S(1)} %copy-done, f32[2,1024]{1,0:T(2,128)S(1)} %copy-done.3), custom_call_target="tpu_custom_call" | custom-call | tf_op jit(solution)/shard_map/pallas_call | solution.py:285
Async XLA Ops:
  0.6 24.1 %copy-start.3 = (f32[2,1024]{1,0:T(2,128)S(1)}, f32[2,1024]{1,0:T(2,128)}, u32[]{:S(2)}) copy-start(f32[2,1024]{1,0:T(2,128)} %accums_ref.1) | copy-start | bytes 24580
  0.6 24.1 %copy-start = (f32[2,1024,256]{2,1,0:T(8,128)S(1)}, f32[2,1024,256]{2,1,0:T(8,128)}, u32[]{:S(2)}) copy-start(f32[2,1024,256]{2,1,0:T(8,128)} %tables_ref.1) | copy-start | bytes 6291460
  24.8 0.9 %copy-start.1 = (f32[2,64,256]{2,1,0:T(8,128)S(1)}, f32[2,64,256]{2,1,0:T(8,128)}, u32[]{:S(2)}) copy-start(f32[2,64,256]{2,1,0:T(8,128)} %get-tuple-element.5.arrived_ref) | copy-start | bytes 393220
  25.7 0.7 %copy-start.2 = (s32[4,2,64]{2,1,0:T(2,128)S(1)}, s32[4,2,64]{2,1,0:T(2,128)}, u32[]{:S(2)}) copy-start(s32[4,2,64]{2,1,0:T(2,128)} %get-tuple-element.4.rows_smem.rows_ref) | copy-start | bytes 6148

commit v3 on v2

--- a/solution.py
+++ b/solution.py
@@ -10,11 +10,12 @@
 learning_rate = 0.1
 epsilon = 1e-08
 MESH = pl.DeviceIdType.MESH
+PIECES = 2
 BLOCKS = 4
 
 
 def exchange_kernel(
-    n_group, n_local, chunk, grads_hbm, index_hbm, rows_hbm, arrived_ref, rows_out_ref,
+    n_group, n_local, chunk, grads_hbm, index_hbm, rows_hbm, packed_ref,
     grads, index, rows, sums, pair, recv, rows_recv, acc,
     grad_sems, index_sem, rows_sem, pair_sems, pair_send_sem, send_sem, recv_sem, row_send_sem, row_recv_sem,
 ):
@@ -174,7 +175,11 @@
         device_id={"group": group, "local": local}, device_id_type=MESH,
     )
     row_wait.wait_recv()
-    rows_out_ref[...] = rows_recv[...]
+    slots = rows.shape[1]
+    packed_ref[2 * slots :, :] = jnp.zeros_like(packed_ref[2 * slots :, :])
+    for g in range(n_group):
+        at = 2 * slots + 2 * g
+        packed_ref[at : at + 2, 0:slots] = rows_recv[g].astype(jnp.float32)
     row_wait.wait_send()
     pair_wait_parts = (BLOCKS - 1) * n_group * (peers - 1)
     pltpu.make_async_remote_copy(
@@ -189,61 +194,65 @@
             total = recv[g * places, t]
             for p in range(1, places):
                 total = total + recv[g * places + p, t]
-            arrived_ref[t, g * capacity : (g + 1) * capacity, :] = total
-
-
-def update_kernel(
-    n_group, rows_smem, rows_ref, arrived_ref, tables_ref, accums_ref, new_tables_hbm, new_accums_ref,
-    picked, fresh, new, out_sems,
-):
+            at = t * slots + g * capacity
+            packed_ref[at : at + capacity, :] = total
+
+
+def update_kernel(n_group, slots, packed_ref, tables_ref, accums_ref, new_tables_hbm, new_accums_ref, new, out_sems):
     group, local = lax.axis_index("group"), lax.axis_index("local")
     n_local = lax.axis_size("local")
     rows_dev, width = tables_ref.shape[1:]
-    slots = arrived_ref.shape[1]
     capacity = slots // n_group
-    base = (group * n_local + local) * rows_dev
+    base = ((group * n_local + local) * rows_dev).astype(jnp.float32)
     slot_at = lax.broadcasted_iota(jnp.int32, (capacity, slots), 0)
     lane_at = lax.broadcasted_iota(jnp.int32, (capacity, slots), 1)
-    diagonal = lax.broadcasted_iota(jnp.int32, (slots, slots), 0) == lax.broadcasted_iota(jnp.int32, (slots, slots), 1)
+    first_at = lax.broadcasted_iota(jnp.int32, (slots, slots), 0)
+    second_at = lax.broadcasted_iota(jnp.int32, (slots, slots), 1)
     row_lane = lax.broadcasted_iota(jnp.int32, (slots, rows_dev), 1).astype(jnp.float32)
-
-    def out(t):
-        return pltpu.make_async_copy(new.at[t, pl.ds(0, rows_dev)], new_tables_hbm.at[t], out_sems.at[t])
-
-    def row_of(t, s):
-        return rows_smem[s // capacity, t, group * capacity + s % capacity]
-
-    for t in range(2):
-        new[t, 0:rows_dev] = tables_ref[t]
-        for s in range(slots):
-            row = row_of(t, s)
-            picked[t, s, :] = tables_ref[t, jnp.where(row < 0, 0, row - base), :]
+    piece = rows_dev // PIECES
+    piece_row = lax.broadcasted_iota(jnp.int32, (piece, 3 * slots), 0).astype(jnp.float32)
+
+    def out(t, i):
+        at = pl.ds(i * piece, piece)
+        return pltpu.make_async_copy(new.at[t, at], new_tables_hbm.at[t, at], out_sems.at[t, i])
+
     for t in range(2):
         columns = []
         for g in range(n_group):
             mine = lane_at == slot_at + group * capacity
-            ids = (rows_ref[g, t : t + 1, :]).astype(jnp.float32)
-            columns.append(jnp.sum(jnp.where(mine, ids, 0.0), axis=1, keepdims=True))
+            at = 2 * slots + 2 * g + t
+            columns.append(jnp.sum(jnp.where(mine, packed_ref[at : at + 1, 0:slots], 0.0), axis=1, keepdims=True))
         column = jnp.concatenate(columns, axis=0)
-        as_row = jnp.sum(jnp.where(diagonal, column, 0.0), axis=0, keepdims=True)
-        same = jnp.where(column == as_row, 1.0, 0.0)
+        column = jnp.where(column < 0.0, -1.0, column - base)
+        as_row = jnp.sum(jnp.where(first_at == second_at, column, 0.0), axis=0, keepdims=True)
+        same = column == as_row
         totals = jnp.dot(
-            same, arrived_ref[t], preferred_element_type=jnp.float32, precision=lax.Precision.HIGHEST
+            jnp.where(same, 1.0, 0.0), packed_ref[t * slots : (t + 1) * slots, :],
+            preferred_element_type=jnp.float32, precision=lax.Precision.HIGHEST,
         )
         squares = jnp.mean(totals * totals, axis=1, keepdims=True)
-        local_row = jnp.where(column < 0.0, -1.0, column - base.astype(jnp.float32))
-        hit = row_lane == local_row
+        hit = row_lane == column
         accums = accums_ref[t : t + 1, :]
         old = jnp.sum(jnp.where(hit, accums, 0.0), axis=1, keepdims=True)
         added = jnp.max(jnp.where(hit, squares, 0.0), axis=0, keepdims=True)
         new_accums_ref[t : t + 1, :] = accums + added
-        fresh[t] = picked[t] - learning_rate * totals / (jnp.sqrt(old + squares) + epsilon)
-        for s in range(slots):
-            row = row_of(t, s)
-            new[t, jnp.where(row < 0, rows_dev, row - base), :] = fresh[t, s, :]
-        out(t).start()
+        change = learning_rate * totals / (jnp.sqrt(old + squares) + epsilon)
+        earlier = jnp.max(jnp.where(same & (first_at < second_at), 1.0, 0.0), axis=0, keepdims=True)
+        target = jnp.where(earlier > 0.0, -1.0, as_row)
+        target = jnp.concatenate([target] * 3, axis=1)
+        high = change.astype(jnp.bfloat16)
+        rest = change - high.astype(jnp.float32)
+        middle = rest.astype(jnp.bfloat16)
+        low = (rest - middle.astype(jnp.float32)).astype(jnp.bfloat16)
+        parts = jnp.concatenate([high, middle, low], axis=0)
+        for i in range(PIECES):
+            at = slice(i * piece, (i + 1) * piece)
+            onehot = jnp.where(piece_row + float(i * piece) == target, 1.0, 0.0).astype(jnp.bfloat16)
+            new[t, at] = tables_ref[t, at] - jnp.dot(onehot, parts, preferred_element_type=jnp.float32)
+            out(t, i).start()
     for t in range(2):
-        out(t).wait()
+        for i in range(PIECES):
+            out(t, i).wait()
 
 
 def local_step(n_group, n_local, lookup_grads, slot_index, unique_rows, tables, accums):
@@ -258,14 +267,11 @@
     vmem = pl.BlockSpec(memory_space=pltpu.VMEM)
     hbm = pl.BlockSpec(memory_space=pltpu.HBM)
     dma = pltpu.SemaphoreType.DMA
-    arrived, rows = pl.pallas_call(
+    packed = pl.pallas_call(
         functools.partial(exchange_kernel, n_group, n_local, chunk),
-        out_shape=(
-            jax.ShapeDtypeStruct((2, slots, width), jnp.float32),
-            jax.ShapeDtypeStruct((n_group, 2, slots), jnp.int32),
-        ),
+        out_shape=jax.ShapeDtypeStruct((2 * slots + -(-2 * n_group // 8) * 8, width), jnp.float32),
         in_specs=[hbm, hbm, hbm],
-        out_specs=(vmem, vmem),
+        out_specs=vmem,
         scratch_shapes=[
             pltpu.VMEM((look, width), jnp.bfloat16),
             pltpu.VMEM((2, look), jnp.int32),
@@ -283,21 +289,19 @@
         cost_estimate=pl.CostEstimate(flops=2 * 2 * look * width * slots * n_local, bytes_accessed=2 * look * width, transcendentals=0),
     )(lookup_grads, slot_index, unique_rows)
     return pl.pallas_call(
-        functools.partial(update_kernel, n_group),
+        functools.partial(update_kernel, n_group, slots),
         out_shape=(
             jax.ShapeDtypeStruct(tables.shape, jnp.float32),
             jax.ShapeDtypeStruct(accums.shape, jnp.float32),
         ),
-        in_specs=[pl.BlockSpec(memory_space=pltpu.SMEM), vmem, vmem, vmem, vmem],
+        in_specs=[vmem, vmem, vmem],
         out_specs=(hbm, vmem),
         scratch_shapes=[
-            pltpu.VMEM((2, slots, width), jnp.float32),
-            pltpu.VMEM((2, slots, width), jnp.float32),
-            pltpu.VMEM((2, rows_dev + 8, width), jnp.float32),
-            dma((2,)),
+            pltpu.VMEM((2, rows_dev, width), jnp.float32),
+            dma((2, PIECES)),
         ],
         compiler_params=pltpu.CompilerParams(vmem_limit_bytes=24 * 2**20),
-    )(rows, rows, arrived, tables, accums)
+    )(packed, tables, accums)
 
 
 def solution(mesh):

time: 30 us -> 28.8 us (0.960)
  local copies, waits for them, and re-layouts: 1.58 us -> 0.91 us
  Pallas kernels: 27.6 us -> 27 us
    unnamed x8 -> x6, local copies, waits for them, and re-layouts: 1.58 us -> 0.91 us
    pallas_call x1, Pallas kernels: 3.5 us -> 2.94 us  [local_step(): pl.pallas_call(functools.partial(update_kernel, n_group, slots), out_shap...]
where the time goes in v3:
time: 28.8 us; the launch traced here: 28.6 us
  Pallas kernels  27 us (94%)
  local copies, waits for them, and re-layouts  0.91 us (3%)
  between operations  0.68 us (2%)
    pallas_call x1, Pallas kernels, local_step(): pl.pallas_call(functools.partial(exchange_kernel, n_group, n_local, chunk...  24.1 us
    pallas_call x1, Pallas kernels, local_step(): pl.pallas_call(functools.partial(update_kernel, n_group, slots), out_shap...  2.94 us
    unnamed x6, local copies, waits for them, and re-layouts  0.91 us

profile of v3, /device:TPU:0, one launch (start us, length us, event | category | flops | bytes accessed | tf_op | source)
XLA Modules:
  0.0 28.6 jit_solution(8011367979524629492)
XLA Ops:
  0.6 0.0 copy-start.2
  0.6 0.0 copy-start
  0.7 24.1 %shard_map.68.packed_ref = f32[136,256]{1,0:T(8,128)} custom-call(bf16[8192,256]{1,0:T(8,128)(2,1)} %grads_hbm.1, s32[2,8192]{1,0:T(2,128)} %index_hbm.1, s32[2,64]{1,0:T(2,128)} %rows_hbm.1), custom_call_target="tpu_custom_call" | custom-call | flops 4294967296 | bytes 4194304 | tf_op jit(solution)/shard_map/pallas_call | solution.py:270
  24.8 0.0 copy-done.2
  24.8 0.0 copy-done
  24.8 0.0 copy-start.1
  24.8 0.9 %copy-done.1 = f32[136,256]{1,0:T(8,128)S(1)} copy-done((f32[136,256]{1,0:T(8,128)S(1)}, f32[136,256]{1,0:T(8,128)}, u32[]{:S(2)}) %copy-start.1) | copy-done | bytes 139288
  25.7 2.9 %shard_map.69 = (f32[2,1024,256]{2,1,0:T(8,128)}, f32[2,1024]{1,0:T(2,128)}) custom-call(f32[136,256]{1,0:T(8,128)S(1)} %copy-done.1, f32[2,1024,256]{2,1,0:T(8,128)S(1)} %copy-done, f32[2,1024]{1,0:T(2,128)S(1)} %copy-done.2), custom_call_target="tpu_custom_call" | custom-call | tf_op jit(solution)/shard_map/pallas_call | solution.py:291
Async XLA Ops:
  0.6 24.1 %copy-start.2 = (f32[2,1024]{1,0:T(2,128)S(1)}, f32[2,1024]{1,0:T(2,128)}, u32[]{:S(2)}) copy-start(f32[2,1024]{1,0:T(2,128)} %accums_ref.1) | copy-start | bytes 24580
  0.6 24.1 %copy-start = (f32[2,1024,256]{2,1,0:T(8,128)S(1)}, f32[2,1024,256]{2,1,0:T(8,128)}, u32[]{:S(2)}) copy-start(f32[2,1024,256]{2,1,0:T(8,128)} %tables_ref.1) | copy-start | bytes 6291460
  24.8 0.9 %copy-start.1 = (f32[136,256]{1,0:T(8,128)S(1)}, f32[136,256]{1,0:T(8,128)}, u32[]{:S(2)}) copy-start(f32[136,256]{1,0:T(8,128)} %shard_map.68.packed_ref) | copy-start | bytes 417796

commit v4 on v3

--- a/solution.py
+++ b/solution.py
@@ -115,7 +115,7 @@
 
         lax.fori_loop(0, (peers - 1) * n_group, one, 0)
 
-    def pass_on(step):
+    def pass_on(step, start, stop):
         block = block_at(step)
         mine = block * peers + peer_me
 
@@ -134,7 +134,7 @@
             send_bucket(mine, h, order[step] - 1).start()
             return c
 
-        lax.fori_loop(0, n_group, one, 0)
+        lax.fori_loop(start, stop, one, 0)
 
     sum_block(0)
     pl.semaphore_wait(barrier, n_dev - 1)
@@ -149,7 +149,9 @@
     for step in range(1, BLOCKS - 1):
         sum_block(step)
         start_pairs(step)
-    pass_on(0)
+        if step == 1:
+            pass_on(0, 0, n_group // 2)
+    pass_on(0, n_group // 2, n_group)
     sum_block(BLOCKS - 1)
 
     def own_step(i, c):
@@ -159,7 +161,7 @@
 
     lax.fori_loop(1, buckets, own_step, 0)
     for step in range(1, BLOCKS - 1):
-        pass_on(step)
+        pass_on(step, 0, n_group)
 
     recv[group * places + BLOCKS - 1 + peer_me] = sums[local * n_group + group]
     rows_recv[group] = rows[...]

time: 28.8 us -> 27.7 us (0.962)
  Pallas kernels: 27 us -> 26 us
    pallas_call x1, Pallas kernels: 24.1 us -> 23 us  [local_step(): pl.pallas_call(functools.partial(exchange_kernel, n_group, n_local, chunk...]
where the time goes in v4:
time: 27.7 us; the launch traced here: 27.6 us
  Pallas kernels  26 us (94%)
  local copies, waits for them, and re-layouts  0.91 us (3%)
  between operations  0.68 us (2%)
    pallas_call x1, Pallas kernels, local_step(): pl.pallas_call(functools.partial(exchange_kernel, n_group, n_local, chunk...  23 us
    pallas_call x1, Pallas kernels, local_step(): pl.pallas_call(functools.partial(update_kernel, n_group, slots), out_shap...  2.94 us
    unnamed x6, local copies, waits for them, and re-layouts  0.91 us

profile of v4, /device:TPU:0, one launch (start us, length us, event | category | flops | bytes accessed | tf_op | source)
XLA Modules:
  0.0 27.6 jit_solution(16879605417167782270)
XLA Ops:
  0.6 0.0 copy-start.2
  0.6 0.0 copy-start
  0.7 23.0 %shard_map.68.packed_ref = f32[136,256]{1,0:T(8,128)} custom-call(bf16[8192,256]{1,0:T(8,128)(2,1)} %grads_hbm.1, s32[2,8192]{1,0:T(2,128)} %index_hbm.1, s32[2,64]{1,0:T(2,128)} %rows_hbm.1), custom_call_target="tpu_custom_call" | custom-call | flops 4294967296 | bytes 4194304 | tf_op jit(solution)/shard_map/pallas_call | solution.py:272
  23.7 0.0 copy-done.2
  23.7 0.0 copy-done
  23.7 0.0 copy-start.1
  23.7 0.9 %copy-done.1 = f32[136,256]{1,0:T(8,128)S(1)} copy-done((f32[136,256]{1,0:T(8,128)S(1)}, f32[136,256]{1,0:T(8,128)}, u32[]{:S(2)}) %copy-start.1) | copy-done | bytes 139288
  24.6 2.9 %shard_map.69 = (f32[2,1024,256]{2,1,0:T(8,128)}, f32[2,1024]{1,0:T(2,128)}) custom-call(f32[136,256]{1,0:T(8,128)S(1)} %copy-done.1, f32[2,1024,256]{2,1,0:T(8,128)S(1)} %copy-done, f32[2,1024]{1,0:T(2,128)S(1)} %copy-done.2), custom_call_target="tpu_custom_call" | custom-call | tf_op jit(solution)/shard_map/pallas_call | solution.py:293
Async XLA Ops:
  0.6 23.1 %copy-start.2 = (f32[2,1024]{1,0:T(2,128)S(1)}, f32[2,1024]{1,0:T(2,128)}, u32[]{:S(2)}) copy-start(f32[2,1024]{1,0:T(2,128)} %accums_ref.1) | copy-start | bytes 24580
  0.6 23.1 %copy-start = (f32[2,1024,256]{2,1,0:T(8,128)S(1)}, f32[2,1024,256]{2,1,0:T(8,128)}, u32[]{:S(2)}) copy-start(f32[2,1024,256]{2,1,0:T(8,128)} %tables_ref.1) | copy-start | bytes 6291460
  23.7 0.9 %copy-start.1 = (f32[136,256]{1,0:T(8,128)S(1)}, f32[136,256]{1,0:T(8,128)}, u32[]{:S(2)}) copy-start(f32[136,256]{1,0:T(8,128)} %shard_map.68.packed_ref) | copy-start | bytes 417796
